TPU v7x, 512 devices: a whole 4x4x16 slice. The times are simulated.
512 devices in a mesh: segment: 16 (over x_hi, y, core), row: 32 (over x_lo, z).
Axes of the slice: x: 4 (x_hi: 2, x_lo: 2; x = x_hi * 2 + x_lo), y: 4, z: 16, core: 2. Of those that a mesh axis runs over, the one named last changes fastest.
Arguments:
- image_slabs: float32 [2, 64, 64, 128], P(None, 'row'), may hold values from -6 to 6
- first_kernel: float32 [16, 3, 3, 128, 128], P('segment'), may hold values from -0.1875 to 0.1875
- second_kernel: float32 [16, 3, 3, 128, 128], P('segment'), may hold values from -0.1875 to 0.1875
- skip_kernel: float32 [8, 128, 128], replicated, may hold values from -0.5 to 0.5
- first_gain: float32 [16, 128], P('segment'), may hold values from 0.5 to 2
- first_bias: float32 [16, 128], P('segment'), may hold values from -1.5 to 1.5
- second_gain: float32 [16, 128], P('segment'), may hold values from 0.5 to 2
- second_bias: float32 [16, 128], P('segment'), may hold values from -1.5 to 1.5
Outputs:
- level_out: float32 [2, 64, 64, 128], P(None, 'row', 'segment')
All inputs are finite; a program needn't handle non-finite values.
Results may differ from a plain program's by a relative error of at most 0.00018.
Values sent between devices are 32-bit elements; how exact they have to be, the bound alone decides.
A program may use at most 64 MiB of HBM per device.

v0:
```python
import jax
import jax.numpy as jnp
from jax import lax
from jax.sharding import PartitionSpec as P


def with_halo(cells, sides, width):
    for axis, dim in sides:
        count = lax.axis_size(axis)
        ends = count - 1
        head = lax.slice_in_dim(cells, 0, width, axis=dim)
        tail = lax.slice_in_dim(cells, cells.shape[dim] - width, cells.shape[dim], axis=dim)
        cells = jnp.concatenate(
            [
                lax.ppermute(tail, axis, [(i, (i + 1) % count) for i in range(ends)]),
                cells,
                lax.ppermute(head, axis, [((i + 1) % count, i) for i in range(ends)]),
            ],
            axis=dim,
        )
    return cells


def from_behind(block, axis, distance):
    devices = range(lax.axis_size(axis))
    route = [(i - distance, i) for i in devices if i - distance in devices]
    return lax.ppermute(block, axis, route)


def cut_along(array, dim, devices):
    before, after = (array.shape[:dim], array.shape[dim + 1 :])
    return jnp.moveaxis(array.reshape(*before, devices, -1, *after), dim, 0)


def summed_on_arrival(array, axis, dim):
    devices = lax.axis_size(axis)
    tiles = lax.all_to_all(cut_along(array, dim, devices), axis, 0, 0, tiled=True)
    return jnp.sum(tiles, axis=0)


def convolve_rows(extended, kernel, height):
    breadth = extended.shape[1]
    channels = extended.shape[2]
    padded = jnp.pad(extended, ((0, 0), (1, 1), (0, 0)))
    summed = jnp.zeros((height * breadth, kernel.shape[3]), jnp.float32)
    for row_step in range(3):
        for col_step in range(3):
            window = padded[row_step : row_step + height, col_step : col_step + breadth].reshape(
                height * breadth, channels
            )
            summed = summed + jnp.dot(
                window,
                kernel[row_step, col_step],
                precision=lax.Precision.HIGHEST,
                preferred_element_type=jnp.float32,
            )
    return summed.reshape(height, breadth, kernel.shape[3])


def run_section(current, kernel_one, kernel_two, gain_one, bias_one, gain_two, bias_two, skip_term):
    height = current.shape[0]
    extended = with_halo(current, (("row", 0),), 2)
    hidden = jax.nn.silu(gain_one * convolve_rows(extended, kernel_one, height + 2) + bias_one)
    position = (
        lax.axis_index("row") * height - 1 + lax.broadcasted_iota(jnp.int32, (height + 2, 1, 1), 0)
    )
    inside = (position >= 0) & (position < height * lax.axis_size("row"))
    hidden = jnp.where(inside, hidden, 0.0)
    second_pre = convolve_rows(hidden, kernel_two, height)
    return current + jax.nn.silu(gain_two * (second_pre + skip_term) + bias_two)


def on_device(
    image_slabs,
    first_kernel,
    second_kernel,
    skip_kernel,
    first_gain,
    first_bias,
    second_gain,
    second_bias,
):
    segment_index = lax.axis_index("segment")
    segment_count = lax.axis_size("segment")
    half_count = segment_count // 2
    micro_count = image_slabs.shape[0]
    height = image_slabs.shape[1]
    breadth = image_slabs.shape[2]
    channels = image_slabs.shape[3]
    kernel_one = first_kernel[0]
    kernel_two = second_kernel[0]
    gain_one = first_gain[0]
    bias_one = first_bias[0]
    gain_two = second_gain[0]
    bias_two = second_bias[0]
    decoder = segment_index >= half_count
    own_skip = lax.dynamic_index_in_dim(
        skip_kernel, jnp.clip(segment_index - half_count, 0, half_count - 1), 0, keepdims=False
    )
    mirror_slot = jnp.clip(segment_count - 1 - segment_index, 0, half_count - 1)
    own_slot = jnp.clip(segment_index, 0, half_count - 1)
    empty_slab = jnp.zeros((height, breadth, channels), jnp.float32)
    results = jnp.zeros((micro_count, height, breadth, channels), jnp.float32)
    skip_store = jnp.zeros((half_count, height, breadth, channels), jnp.float32)

    def advance(moment, carried_state):
        incoming, skip_store, results = carried_state
        micro_item = moment - segment_index
        active = (micro_item >= 0) & (micro_item < micro_count)
        micro_slot = jnp.clip(micro_item, 0, micro_count - 1)
        arriving = lax.dynamic_index_in_dim(
            image_slabs, jnp.clip(moment, 0, micro_count - 1), 0, keepdims=False
        )
        current = jnp.where(segment_index == 0, arriving, incoming)
        skip_input = lax.dynamic_index_in_dim(skip_store, mirror_slot, 0, keepdims=False)
        skip_term = jnp.dot(
            skip_input.reshape(height * breadth, channels),
            own_skip,
            precision=lax.Precision.HIGHEST,
            preferred_element_type=jnp.float32,
        ).reshape(height, breadth, channels)
        skip_term = jnp.where(decoder, skip_term, 0.0)
        produced = run_section(
            current, kernel_one, kernel_two, gain_one, bias_one, gain_two, bias_two, skip_term
        )
        results = jnp.where(
            active & (segment_index == segment_count - 1),
            lax.dynamic_update_index_in_dim(results, produced, micro_slot, 0),
            results,
        )
        skip_store = jnp.where(
            decoder, skip_store, lax.dynamic_update_index_in_dim(skip_store, produced, own_slot, 0)
        )
        incoming, skip_store = from_behind((produced, skip_store), "segment", 1)
        return (incoming, skip_store, results)

    carried_state = lax.fori_loop(
        0, micro_count + segment_count - 1, advance, (empty_slab, skip_store, results)
    )
    finished = jnp.where(segment_index == segment_count - 1, carried_state[2], 0.0)
    return summed_on_arrival(finished, "segment", 2)


def solution(mesh):
    placed = (
        P(None, "row", None, None),
        P("segment", None, None, None, None),
        P("segment", None, None, None, None),
        P(),
        P("segment", None),
        P("segment", None),
        P("segment", None),
        P("segment", None),
    )
    return jax.shard_map(
        on_device,
        mesh=mesh,
        in_specs=placed,
        out_specs=P(None, "row", "segment", None),
        check_vma=False,
    )
```

profile of v0, /device:TPU:3, one launch (start us, length us, event | category | flops | bytes accessed | tf_op | source)
XLA Modules:
  0.0 548.4 jit_solution(14430749562015641082)
XLA Ops:
  2.0 504.9 %while.21 = (s32[]{:T(128)}, f32[2,64,128]{2,1,0:T(8,128)S(1)}, f32[8,2,64,128]{3,2,1,0:T(8,128)S(1)}, f32[2,2,64,128]{3,2,1,0:T(8,128)S(1)}, pred[]{:T(512)}, /...) while((s32[]{:T(128)}, f32[2,64,128]{2,1,0:T(8,128)S(1)}, ...), condition=%wide.region_1.2_spmd, body=%wide.region_0.1_spmd.sunk | while | flops 705626112 | bytes 16714281 | solution.py:137
  2.1 11.1 %collective-permute-start = (f32[2,64,128]{2,1,0:T(8,128)S(1)}, f32[2,64,128]{2,1,0:T(8,128)S(1)}, u32[]{:S(2)}, u32[]{:S(2)}) collective-permute-start(f32[2,64,128]{2,1,0:T(8,128)S(1)} %bitcast_select_fusion.4), channel_id=1, source_target_pairs={{1,0},{2,1},{3,2},{4,3},{5,4},{6,5},{7,6},{8,7},{9,8},{10,9},{11,1... | collective-permute-start | bytes 196616 | tf_op jit(solution)/shard_map/while/body/eval_jaxpr/ppermute | solution.py:17
  15.2 5.1 collective-permute-done.1
  26.1 5.2 collective-permute-start.3
  53.0 5.5 %collective-permute-start.3 = (f32[8,2,64,128]{3,2,1,0:T(8,128)S(1)}, f32[8,2,64,128]{3,2,1,0:T(8,128)S(1)}, u32[]{:S(2)}, u32[]{:S(2)}) collective-permute-start(f32[8,2,64,128]{3,2,1,0:T(8,128)S(1)} %get-tuple-element.705), channel_id=1, source_target_pairs={{0,32},{32,64},{64,96},{96,128},{128,160},{160,192},{192,224},{224... | collective-permute-start | bytes 1572872 | tf_op jit(solution)/shard_map/while/body/eval_jaxpr/ppermute | solution.py:27
  80.2 5.5 %collective-permute-start.3 = (f32[8,2,64,128]{3,2,1,0:T(8,128)S(1)}, f32[8,2,64,128]{3,2,1,0:T(8,128)S(1)}, u32[]{:S(2)}, u32[]{:S(2)}) collective-permute-start(f32[8,2,64,128]{3,2,1,0:T(8,128)S(1)} %get-tuple-element.705), channel_id=1, source_target_pairs={{0,32},{32,64},{64,96},{96,128},{128,160},{160,192},{192,224},{224... | collective-permute-start | bytes 1572872 | tf_op jit(solution)/shard_map/while/body/eval_jaxpr/ppermute | solution.py:27
  107.5 5.5 %collective-permute-start.3 = (f32[8,2,64,128]{3,2,1,0:T(8,128)S(1)}, f32[8,2,64,128]{3,2,1,0:T(8,128)S(1)}, u32[]{:S(2)}, u32[]{:S(2)}) collective-permute-start(f32[8,2,64,128]{3,2,1,0:T(8,128)S(1)} %get-tuple-element.705), channel_id=1, source_target_pairs={{0,32},{32,64},{64,96},{96,128},{128,160},{160,192},{192,224},{224... | collective-permute-start | bytes 1572872 | tf_op jit(solution)/shard_map/while/body/eval_jaxpr/ppermute | solution.py:27
  134.7 5.5 %collective-permute-start.3 = (f32[8,2,64,128]{3,2,1,0:T(8,128)S(1)}, f32[8,2,64,128]{3,2,1,0:T(8,128)S(1)}, u32[]{:S(2)}, u32[]{:S(2)}) collective-permute-start(f32[8,2,64,128]{3,2,1,0:T(8,128)S(1)} %get-tuple-element.705), channel_id=1, source_target_pairs={{0,32},{32,64},{64,96},{96,128},{128,160},{160,192},{192,224},{224... | collective-permute-start | bytes 1572872 | tf_op jit(solution)/shard_map/while/body/eval_jaxpr/ppermute | solution.py:27
  161.9 5.5 %collective-permute-start.3 = (f32[8,2,64,128]{3,2,1,0:T(8,128)S(1)}, f32[8,2,64,128]{3,2,1,0:T(8,128)S(1)}, u32[]{:S(2)}, u32[]{:S(2)}) collective-permute-start(f32[8,2,64,128]{3,2,1,0:T(8,128)S(1)} %get-tuple-element.705), channel_id=1, source_target_pairs={{0,32},{32,64},{64,96},{96,128},{128,160},{160,192},{192,224},{224... | collective-permute-start | bytes 1572872 | tf_op jit(solution)/shard_map/while/body/eval_jaxpr/ppermute | solution.py:27
  189.2 6.2 %collective-permute-start.3 = (f32[8,2,64,128]{3,2,1,0:T(8,128)S(1)}, f32[8,2,64,128]{3,2,1,0:T(8,128)S(1)}, u32[]{:S(2)}, u32[]{:S(2)}) collective-permute-start(f32[8,2,64,128]{3,2,1,0:T(8,128)S(1)} %get-tuple-element.705), channel_id=1, source_target_pairs={{0,32},{32,64},{64,96},{96,128},{128,160},{160,192},{192,224},{224... | collective-permute-start | bytes 1572872 | tf_op jit(solution)/shard_map/while/body/eval_jaxpr/ppermute | solution.py:27
  217.1 5.5 %collective-permute-start.3 = (f32[8,2,64,128]{3,2,1,0:T(8,128)S(1)}, f32[8,2,64,128]{3,2,1,0:T(8,128)S(1)}, u32[]{:S(2)}, u32[]{:S(2)}) collective-permute-start(f32[8,2,64,128]{3,2,1,0:T(8,128)S(1)} %get-tuple-element.705), channel_id=1, source_target_pairs={{0,32},{32,64},{64,96},{96,128},{128,160},{160,192},{192,224},{224... | collective-permute-start | bytes 1572872 | tf_op jit(solution)/shard_map/while/body/eval_jaxpr/ppermute | solution.py:27
  244.3 9.1 %collective-permute-start.3 = (f32[8,2,64,128]{3,2,1,0:T(8,128)S(1)}, f32[8,2,64,128]{3,2,1,0:T(8,128)S(1)}, u32[]{:S(2)}, u32[]{:S(2)}) collective-permute-start(f32[8,2,64,128]{3,2,1,0:T(8,128)S(1)} %get-tuple-element.705), channel_id=1, source_target_pairs={{0,32},{32,64},{64,96},{96,128},{128,160},{160,192},{192,224},{224... | collective-permute-start | bytes 1572872 | tf_op jit(solution)/shard_map/while/body/eval_jaxpr/ppermute | solution.py:27
  253.4 4.8 collective-permute-start.2
  275.1 9.1 %collective-permute-start.3 = (f32[8,2,64,128]{3,2,1,0:T(8,128)S(1)}, f32[8,2,64,128]{3,2,1,0:T(8,128)S(1)}, u32[]{:S(2)}, u32[]{:S(2)}) collective-permute-start(f32[8,2,64,128]{3,2,1,0:T(8,128)S(1)} %get-tuple-element.705), channel_id=1, source_target_pairs={{0,32},{32,64},{64,96},{96,128},{128,160},{160,192},{192,224},{224... | collective-permute-start | bytes 1572872 | tf_op jit(solution)/shard_map/while/body/eval_jaxpr/ppermute | solution.py:27
  306.0 9.2 %collective-permute-start.3 = (f32[8,2,64,128]{3,2,1,0:T(8,128)S(1)}, f32[8,2,64,128]{3,2,1,0:T(8,128)S(1)}, u32[]{:S(2)}, u32[]{:S(2)}) collective-permute-start(f32[8,2,64,128]{3,2,1,0:T(8,128)S(1)} %get-tuple-element.705), channel_id=1, source_target_pairs={{0,32},{32,64},{64,96},{96,128},{128,160},{160,192},{192,224},{224... | collective-permute-start | bytes 1572872 | tf_op jit(solution)/shard_map/while/body/eval_jaxpr/ppermute | solution.py:27
  315.1 4.8 collective-permute-start.2
  336.8 9.2 %collective-permute-start.3 = (f32[8,2,64,128]{3,2,1,0:T(8,128)S(1)}, f32[8,2,64,128]{3,2,1,0:T(8,128)S(1)}, u32[]{:S(2)}, u32[]{:S(2)}) collective-permute-start(f32[8,2,64,128]{3,2,1,0:T(8,128)S(1)} %get-tuple-element.705), channel_id=1, source_target_pairs={{0,32},{32,64},{64,96},{96,128},{128,160},{160,192},{192,224},{224... | collective-permute-start | bytes 1572872 | tf_op jit(solution)/shard_map/while/body/eval_jaxpr/ppermute | solution.py:27
  367.6 9.2 %collective-permute-start.3 = (f32[8,2,64,128]{3,2,1,0:T(8,128)S(1)}, f32[8,2,64,128]{3,2,1,0:T(8,128)S(1)}, u32[]{:S(2)}, u32[]{:S(2)}) collective-permute-start(f32[8,2,64,128]{3,2,1,0:T(8,128)S(1)} %get-tuple-element.705), channel_id=1, source_target_pairs={{0,32},{32,64},{64,96},{96,128},{128,160},{160,192},{192,224},{224... | collective-permute-start | bytes 1572872 | tf_op jit(solution)/shard_map/while/body/eval_jaxpr/ppermute | solution.py:27
  376.8 4.8 collective-permute-start.2
  398.5 9.1 %collective-permute-start.3 = (f32[8,2,64,128]{3,2,1,0:T(8,128)S(1)}, f32[8,2,64,128]{3,2,1,0:T(8,128)S(1)}, u32[]{:S(2)}, u32[]{:S(2)}) collective-permute-start(f32[8,2,64,128]{3,2,1,0:T(8,128)S(1)} %get-tuple-element.705), channel_id=1, source_target_pairs={{0,32},{32,64},{64,96},{96,128},{128,160},{160,192},{192,224},{224... | collective-permute-start | bytes 1572872 | tf_op jit(solution)/shard_map/while/body/eval_jaxpr/ppermute | solution.py:27
  429.3 9.2 %collective-permute-start.3 = (f32[8,2,64,128]{3,2,1,0:T(8,128)S(1)}, f32[8,2,64,128]{3,2,1,0:T(8,128)S(1)}, u32[]{:S(2)}, u32[]{:S(2)}) collective-permute-start(f32[8,2,64,128]{3,2,1,0:T(8,128)S(1)} %get-tuple-element.705), channel_id=1, source_target_pairs={{0,32},{32,64},{64,96},{96,128},{128,160},{160,192},{192,224},{224... | collective-permute-start | bytes 1572872 | tf_op jit(solution)/shard_map/while/body/eval_jaxpr/ppermute | solution.py:27
  460.2 9.1 %collective-permute-start.3 = (f32[8,2,64,128]{3,2,1,0:T(8,128)S(1)}, f32[8,2,64,128]{3,2,1,0:T(8,128)S(1)}, u32[]{:S(2)}, u32[]{:S(2)}) collective-permute-start(f32[8,2,64,128]{3,2,1,0:T(8,128)S(1)} %get-tuple-element.705), channel_id=1, source_target_pairs={{0,32},{32,64},{64,96},{96,128},{128,160},{160,192},{192,224},{224... | collective-permute-start | bytes 1572872 | tf_op jit(solution)/shard_map/while/body/eval_jaxpr/ppermute | solution.py:27
  490.9 9.2 %collective-permute-start.3 = (f32[8,2,64,128]{3,2,1,0:T(8,128)S(1)}, f32[8,2,64,128]{3,2,1,0:T(8,128)S(1)}, u32[]{:S(2)}, u32[]{:S(2)}) collective-permute-start(f32[8,2,64,128]{3,2,1,0:T(8,128)S(1)} %get-tuple-element.705), channel_id=1, source_target_pairs={{0,32},{32,64},{64,96},{96,128},{128,160},{160,192},{192,224},{224... | collective-permute-start | bytes 1572872 | tf_op jit(solution)/shard_map/while/body/eval_jaxpr/ppermute | solution.py:27
  506.9 40.8 %all_to_all.5 = f32[16,2,2,4,128]{4,3,2,1,0:T(4,128)S(1)} all-to-all(f32[16,2,2,4,128]{4,3,2,1,0:T(4,128)S(1)} %copy.9), channel_id=1, replica_groups=mesh['segment'=16,'row'=32] {'segment'}, dimensions={0} | all-to-all | bytes 262144 | tf_op jit(solution)/shard_map/all_to_all | solution.py:37
  (645 shorter events, 345.4 us)
Async XLA Ops:
  2.1 13.1 %collective-permute-start = (f32[2,64,128]{2,1,0:T(8,128)S(1)}, f32[2,64,128]{2,1,0:T(8,128)S(1)}, u32[]{:S(2)}, u32[]{:S(2)}) collective-permute-start(f32[2,64,128]{2,1,0:T(8,128)S(1)} %bitcast_select_fusion.4), channel_id=1, source_target_pairs={{1,0},{2,1},{3,2},{4,3},{5,4},{6,5},{7,6},{8,7},{9,8},{10,9},{11,1... | collective-permute-start | bytes 196616 | tf_op jit(solution)/shard_map/while/body/eval_jaxpr/ppermute | solution.py:17
  13.2 7.1 %collective-permute-start.1 = (f32[2,64,128]{2,1,0:T(8,128)S(1)}, f32[2,64,128]{2,1,0:T(8,128)S(1)}, u32[]{:S(2)}, u32[]{:S(2)}) collective-permute-start(f32[2,64,128]{2,1,0:T(8,128)S(1)} %bitcast_select_fusion.4), channel_id=1, source_target_pairs={{0,1},{1,2},{2,3},{3,4},{4,5},{5,6},{6,7},{7,8},{8,9},{9,10},{10,1... | collective-permute-start | bytes 196616 | tf_op jit(solution)/shard_map/while/body/eval_jaxpr/ppermute | solution.py:15
  26.1 11.3 %collective-permute-start.3 = (f32[8,2,64,128]{3,2,1,0:T(8,128)S(1)}, f32[8,2,64,128]{3,2,1,0:T(8,128)S(1)}, u32[]{:S(2)}, u32[]{:S(2)}) collective-permute-start(f32[8,2,64,128]{3,2,1,0:T(8,128)S(1)} %get-tuple-element.705), channel_id=1, source_target_pairs={{0,32},{32,64},{64,96},{96,128},{128,160},{160,192},{192,224},{224... | collective-permute-start | bytes 1572872 | tf_op jit(solution)/shard_map/while/body/eval_jaxpr/ppermute | solution.py:27
  53.0 11.7 %collective-permute-start.3 = (f32[8,2,64,128]{3,2,1,0:T(8,128)S(1)}, f32[8,2,64,128]{3,2,1,0:T(8,128)S(1)}, u32[]{:S(2)}, u32[]{:S(2)}) collective-permute-start(f32[8,2,64,128]{3,2,1,0:T(8,128)S(1)} %get-tuple-element.705), channel_id=1, source_target_pairs={{0,32},{32,64},{64,96},{96,128},{128,160},{160,192},{192,224},{224... | collective-permute-start | bytes 1572872 | tf_op jit(solution)/shard_map/while/body/eval_jaxpr/ppermute | solution.py:27
  67.3 7.1 %collective-permute-start.1 = (f32[2,64,128]{2,1,0:T(8,128)S(1)}, f32[2,64,128]{2,1,0:T(8,128)S(1)}, u32[]{:S(2)}, u32[]{:S(2)}) collective-permute-start(f32[2,64,128]{2,1,0:T(8,128)S(1)} %bitcast_select_fusion.4), channel_id=1, source_target_pairs={{0,1},{1,2},{2,3},{3,4},{4,5},{5,6},{6,7},{7,8},{8,9},{9,10},{10,1... | collective-permute-start | bytes 196616 | tf_op jit(solution)/shard_map/while/body/eval_jaxpr/ppermute | solution.py:15
  80.2 11.7 %collective-permute-start.3 = (f32[8,2,64,128]{3,2,1,0:T(8,128)S(1)}, f32[8,2,64,128]{3,2,1,0:T(8,128)S(1)}, u32[]{:S(2)}, u32[]{:S(2)}) collective-permute-start(f32[8,2,64,128]{3,2,1,0:T(8,128)S(1)} %get-tuple-element.705), channel_id=1, source_target_pairs={{0,32},{32,64},{64,96},{96,128},{128,160},{160,192},{192,224},{224... | collective-permute-start | bytes 1572872 | tf_op jit(solution)/shard_map/while/body/eval_jaxpr/ppermute | solution.py:27
  94.5 7.1 %collective-permute-start.1 = (f32[2,64,128]{2,1,0:T(8,128)S(1)}, f32[2,64,128]{2,1,0:T(8,128)S(1)}, u32[]{:S(2)}, u32[]{:S(2)}) collective-permute-start(f32[2,64,128]{2,1,0:T(8,128)S(1)} %bitcast_select_fusion.4), channel_id=1, source_target_pairs={{0,1},{1,2},{2,3},{3,4},{4,5},{5,6},{6,7},{7,8},{8,9},{9,10},{10,1... | collective-permute-start | bytes 196616 | tf_op jit(solution)/shard_map/while/body/eval_jaxpr/ppermute | solution.py:15
  107.5 11.7 %collective-permute-start.3 = (f32[8,2,64,128]{3,2,1,0:T(8,128)S(1)}, f32[8,2,64,128]{3,2,1,0:T(8,128)S(1)}, u32[]{:S(2)}, u32[]{:S(2)}) collective-permute-start(f32[8,2,64,128]{3,2,1,0:T(8,128)S(1)} %get-tuple-element.705), channel_id=1, source_target_pairs={{0,32},{32,64},{64,96},{96,128},{128,160},{160,192},{192,224},{224... | collective-permute-start | bytes 1572872 | tf_op jit(solution)/shard_map/while/body/eval_jaxpr/ppermute | solution.py:27
  121.8 7.1 %collective-permute-start.1 = (f32[2,64,128]{2,1,0:T(8,128)S(1)}, f32[2,64,128]{2,1,0:T(8,128)S(1)}, u32[]{:S(2)}, u32[]{:S(2)}) collective-permute-start(f32[2,64,128]{2,1,0:T(8,128)S(1)} %bitcast_select_fusion.4), channel_id=1, source_target_pairs={{0,1},{1,2},{2,3},{3,4},{4,5},{5,6},{6,7},{7,8},{8,9},{9,10},{10,1... | collective-permute-start | bytes 196616 | tf_op jit(solution)/shard_map/while/body/eval_jaxpr/ppermute | solution.py:15
  134.7 11.7 %collective-permute-start.3 = (f32[8,2,64,128]{3,2,1,0:T(8,128)S(1)}, f32[8,2,64,128]{3,2,1,0:T(8,128)S(1)}, u32[]{:S(2)}, u32[]{:S(2)}) collective-permute-start(f32[8,2,64,128]{3,2,1,0:T(8,128)S(1)} %get-tuple-element.705), channel_id=1, source_target_pairs={{0,32},{32,64},{64,96},{96,128},{128,160},{160,192},{192,224},{224... | collective-permute-start | bytes 1572872 | tf_op jit(solution)/shard_map/while/body/eval_jaxpr/ppermute | solution.py:27
  149.0 7.1 %collective-permute-start.1 = (f32[2,64,128]{2,1,0:T(8,128)S(1)}, f32[2,64,128]{2,1,0:T(8,128)S(1)}, u32[]{:S(2)}, u32[]{:S(2)}) collective-permute-start(f32[2,64,128]{2,1,0:T(8,128)S(1)} %bitcast_select_fusion.4), channel_id=1, source_target_pairs={{0,1},{1,2},{2,3},{3,4},{4,5},{5,6},{6,7},{7,8},{8,9},{9,10},{10,1... | collective-permute-start | bytes 196616 | tf_op jit(solution)/shard_map/while/body/eval_jaxpr/ppermute | solution.py:15
  161.9 11.7 %collective-permute-start.3 = (f32[8,2,64,128]{3,2,1,0:T(8,128)S(1)}, f32[8,2,64,128]{3,2,1,0:T(8,128)S(1)}, u32[]{:S(2)}, u32[]{:S(2)}) collective-permute-start(f32[8,2,64,128]{3,2,1,0:T(8,128)S(1)} %get-tuple-element.705), channel_id=1, source_target_pairs={{0,32},{32,64},{64,96},{96,128},{128,160},{160,192},{192,224},{224... | collective-permute-start | bytes 1572872 | tf_op jit(solution)/shard_map/while/body/eval_jaxpr/ppermute | solution.py:27
  176.2 7.1 %collective-permute-start.1 = (f32[2,64,128]{2,1,0:T(8,128)S(1)}, f32[2,64,128]{2,1,0:T(8,128)S(1)}, u32[]{:S(2)}, u32[]{:S(2)}) collective-permute-start(f32[2,64,128]{2,1,0:T(8,128)S(1)} %bitcast_select_fusion.4), channel_id=1, source_target_pairs={{0,1},{1,2},{2,3},{3,4},{4,5},{5,6},{6,7},{7,8},{8,9},{9,10},{10,1... | collective-permute-start | bytes 196616 | tf_op jit(solution)/shard_map/while/body/eval_jaxpr/ppermute | solution.py:15
  189.2 12.3 %collective-permute-start.3 = (f32[8,2,64,128]{3,2,1,0:T(8,128)S(1)}, f32[8,2,64,128]{3,2,1,0:T(8,128)S(1)}, u32[]{:S(2)}, u32[]{:S(2)}) collective-permute-start(f32[8,2,64,128]{3,2,1,0:T(8,128)S(1)} %get-tuple-element.705), channel_id=1, source_target_pairs={{0,32},{32,64},{64,96},{96,128},{128,160},{160,192},{192,224},{224... | collective-permute-start | bytes 1572872 | tf_op jit(solution)/shard_map/while/body/eval_jaxpr/ppermute | solution.py:27
  217.1 11.7 %collective-permute-start.3 = (f32[8,2,64,128]{3,2,1,0:T(8,128)S(1)}, f32[8,2,64,128]{3,2,1,0:T(8,128)S(1)}, u32[]{:S(2)}, u32[]{:S(2)}) collective-permute-start(f32[8,2,64,128]{3,2,1,0:T(8,128)S(1)} %get-tuple-element.705), channel_id=1, source_target_pairs={{0,32},{32,64},{64,96},{96,128},{128,160},{160,192},{192,224},{224... | collective-permute-start | bytes 1572872 | tf_op jit(solution)/shard_map/while/body/eval_jaxpr/ppermute | solution.py:27
  244.3 15.2 %collective-permute-start.3 = (f32[8,2,64,128]{3,2,1,0:T(8,128)S(1)}, f32[8,2,64,128]{3,2,1,0:T(8,128)S(1)}, u32[]{:S(2)}, u32[]{:S(2)}) collective-permute-start(f32[8,2,64,128]{3,2,1,0:T(8,128)S(1)} %get-tuple-element.705), channel_id=1, source_target_pairs={{0,32},{32,64},{64,96},{96,128},{128,160},{160,192},{192,224},{224... | collective-permute-start | bytes 1572872 | tf_op jit(solution)/shard_map/while/body/eval_jaxpr/ppermute | solution.py:27
  275.1 15.3 %collective-permute-start.3 = (f32[8,2,64,128]{3,2,1,0:T(8,128)S(1)}, f32[8,2,64,128]{3,2,1,0:T(8,128)S(1)}, u32[]{:S(2)}, u32[]{:S(2)}) collective-permute-start(f32[8,2,64,128]{3,2,1,0:T(8,128)S(1)} %get-tuple-element.705), channel_id=1, source_target_pairs={{0,32},{32,64},{64,96},{96,128},{128,160},{160,192},{192,224},{224... | collective-permute-start | bytes 1572872 | tf_op jit(solution)/shard_map/while/body/eval_jaxpr/ppermute | solution.py:27
  306.0 15.3 %collective-permute-start.3 = (f32[8,2,64,128]{3,2,1,0:T(8,128)S(1)}, f32[8,2,64,128]{3,2,1,0:T(8,128)S(1)}, u32[]{:S(2)}, u32[]{:S(2)}) collective-permute-start(f32[8,2,64,128]{3,2,1,0:T(8,128)S(1)} %get-tuple-element.705), channel_id=1, source_target_pairs={{0,32},{32,64},{64,96},{96,128},{128,160},{160,192},{192,224},{224... | collective-permute-start | bytes 1572872 | tf_op jit(solution)/shard_map/while/body/eval_jaxpr/ppermute | solution.py:27
  336.8 15.3 %collective-permute-start.3 = (f32[8,2,64,128]{3,2,1,0:T(8,128)S(1)}, f32[8,2,64,128]{3,2,1,0:T(8,128)S(1)}, u32[]{:S(2)}, u32[]{:S(2)}) collective-permute-start(f32[8,2,64,128]{3,2,1,0:T(8,128)S(1)} %get-tuple-element.705), channel_id=1, source_target_pairs={{0,32},{32,64},{64,96},{96,128},{128,160},{160,192},{192,224},{224... | collective-permute-start | bytes 1572872 | tf_op jit(solution)/shard_map/while/body/eval_jaxpr/ppermute | solution.py:27
  367.6 15.3 %collective-permute-start.3 = (f32[8,2,64,128]{3,2,1,0:T(8,128)S(1)}, f32[8,2,64,128]{3,2,1,0:T(8,128)S(1)}, u32[]{:S(2)}, u32[]{:S(2)}) collective-permute-start(f32[8,2,64,128]{3,2,1,0:T(8,128)S(1)} %get-tuple-element.705), channel_id=1, source_target_pairs={{0,32},{32,64},{64,96},{96,128},{128,160},{160,192},{192,224},{224... | collective-permute-start | bytes 1572872 | tf_op jit(solution)/shard_map/while/body/eval_jaxpr/ppermute | solution.py:27
  398.5 15.3 %collective-permute-start.3 = (f32[8,2,64,128]{3,2,1,0:T(8,128)S(1)}, f32[8,2,64,128]{3,2,1,0:T(8,128)S(1)}, u32[]{:S(2)}, u32[]{:S(2)}) collective-permute-start(f32[8,2,64,128]{3,2,1,0:T(8,128)S(1)} %get-tuple-element.705), channel_id=1, source_target_pairs={{0,32},{32,64},{64,96},{96,128},{128,160},{160,192},{192,224},{224... | collective-permute-start | bytes 1572872 | tf_op jit(solution)/shard_map/while/body/eval_jaxpr/ppermute | solution.py:27
  429.3 15.3 %collective-permute-start.3 = (f32[8,2,64,128]{3,2,1,0:T(8,128)S(1)}, f32[8,2,64,128]{3,2,1,0:T(8,128)S(1)}, u32[]{:S(2)}, u32[]{:S(2)}) collective-permute-start(f32[8,2,64,128]{3,2,1,0:T(8,128)S(1)} %get-tuple-element.705), channel_id=1, source_target_pairs={{0,32},{32,64},{64,96},{96,128},{128,160},{160,192},{192,224},{224... | collective-permute-start | bytes 1572872 | tf_op jit(solution)/shard_map/while/body/eval_jaxpr/ppermute | solution.py:27
  460.2 15.2 %collective-permute-start.3 = (f32[8,2,64,128]{3,2,1,0:T(8,128)S(1)}, f32[8,2,64,128]{3,2,1,0:T(8,128)S(1)}, u32[]{:S(2)}, u32[]{:S(2)}) collective-permute-start(f32[8,2,64,128]{3,2,1,0:T(8,128)S(1)} %get-tuple-element.705), channel_id=1, source_target_pairs={{0,32},{32,64},{64,96},{96,128},{128,160},{160,192},{192,224},{224... | collective-permute-start | bytes 1572872 | tf_op jit(solution)/shard_map/while/body/eval_jaxpr/ppermute | solution.py:27
  490.9 15.3 %collective-permute-start.3 = (f32[8,2,64,128]{3,2,1,0:T(8,128)S(1)}, f32[8,2,64,128]{3,2,1,0:T(8,128)S(1)}, u32[]{:S(2)}, u32[]{:S(2)}) collective-permute-start(f32[8,2,64,128]{3,2,1,0:T(8,128)S(1)} %get-tuple-element.705), channel_id=1, source_target_pairs={{0,32},{32,64},{64,96},{96,128},{128,160},{160,192},{192,224},{224... | collective-permute-start | bytes 1572872 | tf_op jit(solution)/shard_map/while/body/eval_jaxpr/ppermute | solution.py:27
  (68 other events, 304.3 us)
where the time goes:
time: 553 us; the launch traced here: 548 us
  starting transfers between devices  286 us (52%)
  waiting for transfers between devices  118 us (21%)
  matrix products  75.2 us (14%)
  blocking collectives  40.8 us (7%)
  local copies, waits for them, and re-layouts  20.6 us (4%)
    ppermute x34, starting transfers between devices, from_behind(): return lax.ppermute(block, axis, route)  188 us
    dot_general x306, matrix products, convolve_rows(): jnp.dot(window, kernel[row_step, col_step], precision=lax.Precision.HIGHE...  71.2 us
    ppermute x17, waiting for transfers between devices, with_halo(): lax.ppermute(tail, axis, [(i, (i + 1) % count) for i in range(ends)])  64.4 us
    ppermute x17, starting transfers between devices, with_halo(): lax.ppermute(tail, axis, [(i, (i + 1) % count) for i in range(ends)])  55.7 us
    ppermute x34, waiting for transfers between devices, from_behind(): return lax.ppermute(block, axis, route)  53.6 us
    ppermute x17, starting transfers between devices, with_halo(): lax.ppermute(head, axis, [((i + 1) % count, i) for i in range(ends)])  41.8 us
    all_to_all x1, blocking collectives, summed_on_arrival(): lax.all_to_all(cut_along(array, dim, devices), axis, 0, 0, tiled=True)  40.8 us
    while x51, local copies, waits for them, and re-layouts  16.3 us
  transfers between devices with their start and end apart: 68, of which 51 were waited for; matrix products, arithmetic and copies ran while one was open for 0% of the time, Pallas kernels for 0%

commit v1 on v0

v1 whole, which is shorter than its diff:
```python
import functools

import jax
import jax.numpy as jnp
from jax import lax
from jax.experimental import pallas as pl
from jax.experimental.pallas import tpu as pltpu
from jax.sharding import PartitionSpec as P

MESH = pl.DeviceIdType.MESH
C = 128
TILE = 32
RING = 40
STRIP = 8


def split(x):
    high = x.astype(jnp.bfloat16).astype(jnp.float32)
    return high, x - high


def silu(u):
    return u / (1.0 + jnp.exp(-u))


def level_kernel(
    n_seg,
    n_row,
    img,
    w1,
    w2,
    skipk,
    g1,
    b1,
    g2,
    b2,
    out,
    xbuf,
    xh,
    xl,
    hh,
    hl,
    h1,
    yout,
    fin,
    landed,
    pw1,
    pw2,
    pvec,
    vecs,
    wp,
    ska,
    skb,
    ea,
    eb,
    m0,
    m2,
    wsend,
    wrecv,
    gsend,
    grecv,
    msend,
    mrecv,
    ssend,
    srecv,
    fsend,
    frecv,
):
    stages = n_seg // 2
    mirror = stages // 2
    groups = n_row // 2
    pieces = n_seg // 2
    cw = 2 * TILE // n_seg
    s = lax.axis_index("segment")
    r = lax.axis_index("row")
    m = s // 2
    c = s % 2
    g = r // 2
    half = r % 2
    up = (g > 0).astype(jnp.int32)
    down = (g < groups - 1).astype(jnp.int32)
    valid = 1 + up + down
    inside = {-1: g > 0, 0: g >= 0, 1: g < groups - 1}

    def greet(cond, seg, row):
        @pl.when(cond)
        def _():
            pl.semaphore_signal(barrier, inc=1, device_id=(seg, row), device_id_type=MESH)

    xbuf[...] = jnp.zeros_like(xbuf)

    barrier = pltpu.get_barrier_semaphore()
    greet(s >= 0, s + 1 - 2 * c, r)
    for d in (-1, 0, 1):
        greet(inside[d] & (m > 0), s - 2, r + 2 * d)
        greet(inside[d] & (m > 0), s - 2, r + 1 - 2 * half + 2 * d)
        for q in (0, 1):
            other = 2 * (g + d) + q
            greet(inside[d] & (m == 0) & (other != r), s, other)
    greet(m > mirror, 2 * (stages - m) + c, r)
    greet(m >= mirror, 2 * (stages - 1 - m) + c, r)
    source = 2 * g + s // pieces
    for k in (0, 1):
        last = n_seg - 2 + k
        greet((s != last) | (r != source), last, source)

    one = jnp.int32(1)
    zero = jnp.int32(0)
    expected = (
        1
        + jnp.where(m < stages - 1, 2 * valid, zero)
        + jnp.where(m == 0, 2 * valid - 1, zero)
        + jnp.where((m > 0) & (m < mirror), one, zero)
        + jnp.where(m < mirror, one, zero)
        + jnp.where(m == stages - 1, 2 * pieces - half, zero)
    )
    pl.semaphore_wait(barrier, expected)

    def swaps():
        pairs = [(w1, pw1), (w2, pw2)] + [(v, pvec.at[i]) for i, v in enumerate((g1, b1, g2, b2))]
        return [
            pltpu.make_async_remote_copy(
                src_ref=a,
                dst_ref=b,
                send_sem=wsend.at[i],
                recv_sem=wrecv.at[i],
                device_id=(s + 1 - 2 * c, r),
                device_id_type=MESH,
            )
            for i, (a, b) in enumerate(pairs)
        ]

    swap = swaps()

    def gathers(start):
        for d in (-1, 0, 1):
            for q in (0, 1):
                other = 2 * (g + d) + q
                offset = 2 * half - 4 * d + 4
                index = (2 * (1 - d) + half) * 2
                strip = TILE if q == 0 else TILE - STRIP

                @pl.when((m == 0) & inside[d] & (other != r))
                def _():
                    for kind, (a, b) in enumerate(
                        (
                            (img.at[c, :, TILE * q : TILE * q + TILE, :], (0, TILE)),
                            (img.at[c, :, strip : strip + STRIP, :], (TILE, STRIP)),
                        )
                    ):
                        copy = pltpu.make_async_remote_copy(
                            src_ref=a,
                            dst_ref=xbuf.at[pl.ds(offset, 2), b[0] : b[0] + b[1], :],
                            send_sem=gsend.at[((d + 1) * 2 + q) * 2 + kind],
                            recv_sem=grecv.at[index + kind],
                            device_id=(s, other),
                            device_id_type=MESH,
                        )
                        if start:
                            copy.start()
                        else:
                            copy.wait_send()

    gathers(True)
    for copy in swap:
        copy.start()

    column = lax.broadcasted_iota(jnp.int32, (RING, C), 0)
    m0[...] = jnp.where((column == 0) & (half == 0), 0.0, 1.0)
    m2[...] = jnp.where((column == TILE - 1) & (half == 1), 0.0, 1.0)

    def prepare(slot, conv, ref):
        for a in range(3):
            for b in range(3):
                high, low = split(ref[0, a, b])
                cols = pl.ds(b * C, C)
                wp[slot, conv, pl.ds(a * C, C), cols] = high
                wp[slot, conv, pl.ds((3 + a) * C, C), cols] = high
                wp[slot, conv, pl.ds((6 + a) * C, C), cols] = low

    prepare(c, 0, w1)
    prepare(c, 1, w2)
    for i, v in enumerate((g1, b1, g2, b2)):
        vecs[c, i] = v[...]
    swap[0].wait_recv()
    prepare(1 - c, 0, pw1)
    swap[1].wait_recv()
    prepare(1 - c, 1, pw2)
    for i in range(4):
        swap[2 + i].wait_recv()
        vecs[1 - c, i] = pvec[i]

    def skip_term(src, dst, which):
        rows = src.shape[0]
        xv, xw = split(src[...].reshape(rows * RING, C))
        kh, kl = split(skipk[which])
        dot = functools.partial(jnp.dot, preferred_element_type=jnp.float32)
        term = dot(xv, kh) + (dot(xv, kl) + dot(xw, kh))
        dst[...] = term.reshape(rows, RING, C)

    ea[...] = jnp.zeros_like(ea)
    eb[...] = jnp.zeros_like(eb)

    def forward_a():
        return pltpu.make_async_remote_copy(
            src_ref=xbuf.at[2:10],
            dst_ref=ska,
            send_sem=ssend.at[0],
            recv_sem=srecv.at[0],
            device_id=(2 * (stages - m) + c, r),
            device_id_type=MESH,
        )

    def forward_b():
        return pltpu.make_async_remote_copy(
            src_ref=h1.at[4:8],
            dst_ref=skb,
            send_sem=ssend.at[1],
            recv_sem=srecv.at[1],
            device_id=(2 * (stages - 1 - m) + c, r),
            device_id_type=MESH,
        )

    @pl.when(m > mirror)
    def _():
        forward_a().wait_recv()
        skip_term(ska, ea, jnp.maximum(2 * (m - mirror), 0))

    @pl.when(m >= mirror)
    def _():
        forward_b().wait_recv()
        skip_term(skb, eb, jnp.maximum(2 * (m - mirror) + 1, 0))

    def handover(d, kind):
        slot = 1 - d
        if kind == 0:
            src = yout
            dst = xbuf.at[4 * slot : 4 * slot + 4, 0:TILE, :]
            row = r + 2 * d
        else:
            src = yout.at[:, pl.ds(pl.multiple_of((TILE - STRIP) * (1 - half), STRIP), STRIP), :]
            dst = xbuf.at[4 * slot : 4 * slot + 4, TILE:RING, :]
            row = r + 1 - 2 * half + 2 * d
        return pltpu.make_async_remote_copy(
            src_ref=src,
            dst_ref=dst,
            send_sem=msend.at[2 * (d + 1) + kind],
            recv_sem=mrecv.at[2 * slot + kind],
            device_id=(s + 2, row),
            device_id_type=MESH,
        )

    for d in (-1, 0, 1):

        @pl.when((m == 0) & inside[d])
        def _():
            for p in (0, 1):
                index = (2 * (1 + d) + p) * 2

                @pl.when((2 * (g + d) + p) != r)
                def _():
                    for kind, b in enumerate(((0, TILE), (TILE, STRIP))):
                        rows = 2 * p + 4 * d + 4
                        pltpu.make_async_remote_copy(
                            src_ref=xbuf.at[rows : rows + 2, b[0] : b[0] + b[1], :],
                            dst_ref=xbuf.at[rows : rows + 2, b[0] : b[0] + b[1], :],
                            send_sem=gsend.at[0],
                            recv_sem=grecv.at[index + kind],
                            device_id=(s, r),
                            device_id_type=MESH,
                        ).wait_recv()

        @pl.when((m > 0) & inside[d])
        def _():
            for kind in (0, 1):
                handover(-d, kind).wait_recv()

    for q in (0, 1):

        @pl.when((m == 0) & (half == q))
        def _():
            strip = TILE if q == 0 else TILE - STRIP
            xbuf[4 + 2 * q : 6 + 2 * q, 0:TILE, :] = img[c, :, TILE * q : TILE * q + TILE, :]
            xbuf[4 + 2 * q : 6 + 2 * q, TILE:RING, :] = img[c, :, strip : strip + STRIP, :]

    @pl.when((m > 0) & (m < mirror))
    def _():
        forward_a().start()

    @pl.when(m == mirror)
    def _():
        skip_term(xbuf.at[2:10], ea, 0)

    def conv(high, low, first, rows, slot, which):
        def part(ref, a):
            return ref[first - 1 + a : first - 1 + a + rows].reshape(rows * RING, C)

        hs = [part(high, a) for a in range(3)]
        ls = [part(low, a) for a in range(3)]
        left = jnp.concatenate(hs + ls + hs, axis=1)
        acc = jnp.dot(left, wp[slot, which], preferred_element_type=jnp.float32)
        left_tap, middle, right_tap = [
            acc[:, b * C : (b + 1) * C].reshape(rows, RING, C) for b in range(3)
        ]
        return (
            pltpu.roll(left_tap, 1, 1) * m0[...][None]
            + middle
            + pltpu.roll(right_tap, RING - 1, 1) * m2[...][None]
        )

    def inside_rows(value, first):
        row = 4 * g - 4 + first + lax.broadcasted_iota(jnp.int32, value.shape, 0)
        return jnp.where((row >= 0) & (row < 4 * groups), value, 0.0)

    def vec(slot, i):
        return vecs[slot, i].reshape(1, 1, C)

    def store_split(high, low, first, value):
        top, rest = split(value)
        high[first : first + value.shape[0]] = top
        low[first : first + value.shape[0]] = rest

    store_split(xh, xl, 0, xbuf[...])
    hidden = inside_rows(silu(vec(0, 0) * conv(xh, xl, 1, 10, 0, 0) + vec(0, 1)), 1)
    store_split(hh, hl, 1, hidden)
    value = xbuf[2:10] + silu(vec(0, 2) * (conv(hh, hl, 2, 8, 0, 1) + ea[...]) + vec(0, 3))
    value = inside_rows(value, 2)
    h1[2:10] = value
    store_split(xh, xl, 2, value)

    @pl.when(m < mirror)
    def _():
        forward_b().start()

    hidden = inside_rows(silu(vec(1, 0) * conv(xh, xl, 3, 6, 1, 0) + vec(1, 1)), 3)
    store_split(hh, hl, 3, hidden)
    value = h1[4:8] + silu(vec(1, 2) * (conv(hh, hl, 4, 4, 1, 1) + eb[...]) + vec(1, 3))
    value = value[:, 0:TILE]

    @pl.when(m < stages - 1)
    def _():
        yout[...] = value
        for kind in (0, 1):
            for d in (-1, 1, 0):

                @pl.when(inside[d])
                def _():
                    handover(d, kind).start()

    def scatter(i, p):
        return pltpu.make_async_remote_copy(
            src_ref=fin.at[i, 2 * p : 2 * p + 2],
            dst_ref=landed.at[c],
            send_sem=fsend.at[2 * i + p],
            recv_sem=frecv.at[c],
            device_id=(pieces * half + i, 2 * g + p),
            device_id_type=MESH,
        )

    def each_piece(action):
        for i in range(pieces):
            for p in (0, 1):

                @pl.when((pieces * half + i != s) | (2 * g + p != r))
                def _():
                    action(scatter(i, p))

    @pl.when(m == stages - 1)
    def _():
        for i in range(pieces):
            fin[i] = value[:, i * cw : (i + 1) * cw, :]
        each_piece(lambda copy: copy.start())

        @pl.when(half == 1)
        def _():
            landed[c] = fin[pieces - 2 + c, 2:4]

    for k in (0, 1):

        @pl.when((s != n_seg - 2 + k) | (r != source))
        def _():
            pltpu.make_async_remote_copy(
                src_ref=fin.at[0, 0:2],
                dst_ref=landed.at[k],
                send_sem=fsend.at[0],
                recv_sem=frecv.at[k],
                device_id=(s, r),
                device_id_type=MESH,
            ).wait_recv()

    out[...] = landed[...]

    for copy in swap:
        copy.wait_send()
    gathers(False)

    @pl.when(m < stages - 1)
    def _():
        for kind in (0, 1):
            for d in (-1, 0, 1):

                @pl.when(inside[d])
                def _():
                    handover(d, kind).wait_send()

    @pl.when((m > 0) & (m < mirror))
    def _():
        forward_a().wait_send()

    @pl.when(m < mirror)
    def _():
        forward_b().wait_send()

    @pl.when(m == stages - 1)
    def _():
        each_piece(lambda copy: copy.wait_send())


def solution(mesh):
    n_seg = mesh.shape["segment"]
    n_row = mesh.shape["row"]
    pieces = n_seg // 2
    cw = 2 * TILE // n_seg
    f32 = jnp.float32
    vmem = pl.BlockSpec(memory_space=pltpu.VMEM)

    def on_device(*args):
        dma = pltpu.SemaphoreType.DMA
        return pl.pallas_call(
            functools.partial(level_kernel, n_seg, n_row),
            out_shape=jax.ShapeDtypeStruct((2, 2, cw, C), f32),
            in_specs=[vmem] * 8,
            out_specs=vmem,
            scratch_shapes=[
                pltpu.VMEM((12, RING, C), f32),
                pltpu.VMEM((12, RING, C), f32),
                pltpu.VMEM((12, RING, C), f32),
                pltpu.VMEM((12, RING, C), f32),
                pltpu.VMEM((12, RING, C), f32),
                pltpu.VMEM((12, RING, C), f32),
                pltpu.VMEM((4, TILE, C), f32),
                pltpu.VMEM((pieces, 4, cw, C), f32),
                pltpu.VMEM((2, 2, cw, C), f32),
                pltpu.VMEM((1, 3, 3, C, C), f32),
                pltpu.VMEM((1, 3, 3, C, C), f32),
                pltpu.VMEM((4, 1, C), f32),
                pltpu.VMEM((2, 4, 1, C), f32),
                pltpu.VMEM((2, 2, 9 * C, 3 * C), f32),
                pltpu.VMEM((8, RING, C), f32),
                pltpu.VMEM((4, RING, C), f32),
                pltpu.VMEM((8, RING, C), f32),
                pltpu.VMEM((4, RING, C), f32),
                pltpu.VMEM((RING, C), f32),
                pltpu.VMEM((RING, C), f32),
                dma((6,)),
                dma((6,)),
                dma((12,)),
                dma((12,)),
                dma((6,)),
                dma((6,)),
                dma((2,)),
                dma((2,)),
                dma((2 * pieces,)),
                dma((2,)),
            ],
            compiler_params=pltpu.CompilerParams(
                collective_id=0, has_side_effects=True, vmem_limit_bytes=48 * 1024 * 1024
            ),
        )(*args)

    return jax.shard_map(
        on_device,
        mesh=mesh,
        in_specs=(
            P(None, "row", None, None),
            P("segment", None, None, None, None),
            P("segment", None, None, None, None),
            P(),
            P("segment", None),
            P("segment", None),
            P("segment", None),
            P("segment", None),
        ),
        out_specs=P(None, "row", "segment", None),
        check_vma=False,
    )
```

time: 553 us -> 97 us (0.18)
  the two profiles are of different devices: /device:TPU:3 before, /device:TPU:1 now
where the time goes in v1:
time: 97 us; the launch traced here: 96.7 us
  Pallas kernels  89.4 us (92%)
  local copies, waits for them, and re-layouts  7.29 us (8%)
    pallas_call x1, Pallas kernels, on_device(): pl.pallas_call(functools.partial(level_kernel, n_seg, n_row), out_shape=j...  89.4 us
    unnamed x17, local copies, waits for them, and re-layouts  7.29 us

profile of v1, /device:TPU:1, one launch (start us, length us, event | category | flops | bytes accessed | tf_op | source)
XLA Modules:
  0.0 96.7 jit_solution(11322038122220891643)
XLA Ops:
  0.0 0.0 copy-start
  0.0 1.1 %copy-done = f32[1,3,3,128,128]{4,3,2,1,0:T(8,128)S(1)} copy-done((f32[1,3,3,128,128]{4,3,2,1,0:T(8,128)S(1)}, f32[1,3,3,128,128]{4,3,2,1,0:T(8,128)}, u32[]{:S(2)}) %copy-start) | copy-done | bytes 589848
  1.1 0.0 copy-start.1
  1.1 1.1 %copy-done.1 = f32[1,3,3,128,128]{4,3,2,1,0:T(8,128)S(1)} copy-done((f32[1,3,3,128,128]{4,3,2,1,0:T(8,128)S(1)}, f32[1,3,3,128,128]{4,3,2,1,0:T(8,128)}, u32[]{:S(2)}) %copy-start.1) | copy-done | bytes 589848
  2.1 0.0 copy-start.2
  2.1 1.0 %copy-done.2 = f32[8,128,128]{2,1,0:T(8,128)S(1)} copy-done((f32[8,128,128]{2,1,0:T(8,128)S(1)}, f32[8,128,128]{2,1,0:T(8,128)}, u32[]{:S(2)}) %copy-start.2) | copy-done | bytes 524312
  3.2 0.0 copy-start.3
  3.2 0.9 copy-done.3
  4.1 0.0 copy-start.4
  4.1 0.7 copy-done.4
  4.7 0.0 copy-start.5
  4.7 0.7 copy-done.5
  5.4 0.0 copy-start.6
  5.4 0.7 copy-done.6
  6.0 0.0 copy-start.7
  6.0 0.7 copy-done.7
  6.7 89.4 %shard_map.82 = f32[2,2,4,128]{3,2,1,0:T(4,128)S(1)} custom-call(f32[2,2,64,128]{3,2,1,0:T(8,128)S(1)} %copy-done.3, f32[1,3,3,128,128]{4,3,2,1,0:T(8,128)S(1)} %copy-done, f32[1,3,3,128,128]{4,3,2,1,0:T(8,128)S(1)} %copy-done.1, f32[8,128,128]{2,1,0:T(8,128)S(1)} %copy-done.2, f32[1,128]{1,0:T(1,128)S(1)} %copy-done.4, f32[1,128]{1,0:T(1,128)S(1)} %copy-done.5, ...), custom_call_target="tpu_custom_call" | custom-call | tf_op jit(solution)/shard_map/pallas_call | solution.py:429
  96.1 0.6 copy.10
Async XLA Ops:
  0.0 1.1 %copy-start = (f32[1,3,3,128,128]{4,3,2,1,0:T(8,128)S(1)}, f32[1,3,3,128,128]{4,3,2,1,0:T(8,128)}, u32[]{:S(2)}) copy-start(f32[1,3,3,128,128]{4,3,2,1,0:T(8,128)} %w1.1) | copy-start | bytes 1769476
  1.1 1.1 %copy-start.1 = (f32[1,3,3,128,128]{4,3,2,1,0:T(8,128)S(1)}, f32[1,3,3,128,128]{4,3,2,1,0:T(8,128)}, u32[]{:S(2)}) copy-start(f32[1,3,3,128,128]{4,3,2,1,0:T(8,128)} %w2.1) | copy-start | bytes 1769476
  2.1 1.0 %copy-start.2 = (f32[8,128,128]{2,1,0:T(8,128)S(1)}, f32[8,128,128]{2,1,0:T(8,128)}, u32[]{:S(2)}) copy-start(f32[8,128,128]{2,1,0:T(8,128)} %skipk.1) | copy-start | bytes 1572868
  3.2 0.9 copy-start.3
  4.1 0.7 copy-start.4
  4.7 0.7 copy-start.5
  5.4 0.7 copy-start.6
  6.0 0.7 copy-start.7

commit v2 on v1

--- a/solution.py
+++ b/solution.py
@@ -26,15 +26,22 @@
 def level_kernel(
     n_seg,
     n_row,
+    img_hbm,
+    w1_hbm,
+    w2_hbm,
+    skipk_hbm,
+    g1_hbm,
+    b1_hbm,
+    g2_hbm,
+    b2_hbm,
+    out,
     img,
     w1,
     w2,
     skipk,
-    g1,
-    b1,
-    g2,
-    b2,
-    out,
+    ovec,
+    sout,
+    sin,
     xbuf,
     xh,
     xl,
@@ -65,6 +72,7 @@
     srecv,
     fsend,
     frecv,
+    lsem,
 ):
     stages = n_seg // 2
     mirror = stages // 2
@@ -76,7 +84,7 @@
     m = s // 2
     c = s % 2
     g = r // 2
-    half = r % 2
+    slab = r % 2
     up = (g > 0).astype(jnp.int32)
     down = (g < groups - 1).astype(jnp.int32)
     valid = 1 + up + down
@@ -87,22 +95,41 @@
         def _():
             pl.semaphore_signal(barrier, inc=1, device_id=(seg, row), device_id_type=MESH)
 
+    first_skip = jnp.maximum(2 * (m - mirror), 0)
+    loads = [
+        pltpu.make_async_copy(a, b, lsem.at[i])
+        for i, (a, b) in enumerate(
+            [
+                (img_hbm, img),
+                (w1_hbm, w1),
+                (w2_hbm, w2),
+                (skipk_hbm.at[pl.ds(first_skip, 2)], skipk),
+                (g1_hbm, ovec.at[0]),
+                (b1_hbm, ovec.at[1]),
+                (g2_hbm, ovec.at[2]),
+                (b2_hbm, ovec.at[3]),
+            ]
+        )
+    ]
+    for copy in loads:
+        copy.start()
+
     xbuf[...] = jnp.zeros_like(xbuf)
+    sin[...] = jnp.zeros_like(sin)
 
     barrier = pltpu.get_barrier_semaphore()
     greet(s >= 0, s + 1 - 2 * c, r)
     for d in (-1, 0, 1):
         greet(inside[d] & (m > 0), s - 2, r + 2 * d)
-        greet(inside[d] & (m > 0), s - 2, r + 1 - 2 * half + 2 * d)
+        greet(inside[d] & (m > 0), s - 1 - 2 * c, r + 2 * d)
         for q in (0, 1):
             other = 2 * (g + d) + q
             greet(inside[d] & (m == 0) & (other != r), s, other)
     greet(m > mirror, 2 * (stages - m) + c, r)
     greet(m >= mirror, 2 * (stages - 1 - m) + c, r)
-    source = 2 * g + s // pieces
+    source = n_seg - 2 + s // pieces
     for k in (0, 1):
-        last = n_seg - 2 + k
-        greet((s != last) | (r != source), last, source)
+        greet((s != source) | (r != 2 * g + k), source, 2 * g + k)
 
     one = jnp.int32(1)
     zero = jnp.int32(0)
@@ -112,12 +139,12 @@
         + jnp.where(m == 0, 2 * valid - 1, zero)
         + jnp.where((m > 0) & (m < mirror), one, zero)
         + jnp.where(m < mirror, one, zero)
-        + jnp.where(m == stages - 1, 2 * pieces - half, zero)
+        + jnp.where(m == stages - 1, 2 * pieces - c, zero)
     )
     pl.semaphore_wait(barrier, expected)
 
     def swaps():
-        pairs = [(w1, pw1), (w2, pw2)] + [(v, pvec.at[i]) for i, v in enumerate((g1, b1, g2, b2))]
+        pairs = [(w1, pw1), (w2, pw2), (ovec, pvec)]
         return [
             pltpu.make_async_remote_copy(
                 src_ref=a,
@@ -132,20 +159,22 @@
 
     swap = swaps()
 
+    own = pl.ds(pl.multiple_of(TILE * c, TILE), TILE)
+    strip = pl.ds(pl.multiple_of(TILE - STRIP * c, STRIP), STRIP)
+
     def gathers(start):
-        for d in (-1, 0, 1):
+        for d in (-1, 1, 0):
             for q in (0, 1):
                 other = 2 * (g + d) + q
-                offset = 2 * half - 4 * d + 4
-                index = (2 * (1 - d) + half) * 2
-                strip = TILE if q == 0 else TILE - STRIP
+                offset = 2 * slab - 4 * d + 4
+                index = (2 * (1 - d) + slab) * 2
 
                 @pl.when((m == 0) & inside[d] & (other != r))
                 def _():
                     for kind, (a, b) in enumerate(
                         (
-                            (img.at[c, :, TILE * q : TILE * q + TILE, :], (0, TILE)),
-                            (img.at[c, :, strip : strip + STRIP, :], (TILE, STRIP)),
+                            (img.at[q, :, own, :], (0, TILE)),
+                            (img.at[q, :, strip, :], (TILE, STRIP)),
                         )
                     ):
                         copy = pltpu.make_async_remote_copy(
@@ -161,13 +190,17 @@
                         else:
                             copy.wait_send()
 
+    loads[0].wait()
     gathers(True)
+
+    for copy in loads[1:]:
+        copy.wait()
     for copy in swap:
         copy.start()
 
     column = lax.broadcasted_iota(jnp.int32, (RING, C), 0)
-    m0[...] = jnp.where((column == 0) & (half == 0), 0.0, 1.0)
-    m2[...] = jnp.where((column == TILE - 1) & (half == 1), 0.0, 1.0)
+    m0[...] = jnp.where((column == 0) & (c == 0), 0.0, 1.0)
+    m2[...] = jnp.where((column == TILE - 1) & (c == 1), 0.0, 1.0)
 
     def prepare(slot, conv, ref):
         for a in range(3):
@@ -180,23 +213,21 @@
 
     prepare(c, 0, w1)
     prepare(c, 1, w2)
-    for i, v in enumerate((g1, b1, g2, b2)):
-        vecs[c, i] = v[...]
+    vecs[c] = ovec[...]
     swap[0].wait_recv()
     prepare(1 - c, 0, pw1)
     swap[1].wait_recv()
     prepare(1 - c, 1, pw2)
-    for i in range(4):
-        swap[2 + i].wait_recv()
-        vecs[1 - c, i] = pvec[i]
+    swap[2].wait_recv()
+    vecs[1 - c] = pvec[...]
 
     def skip_term(src, dst, which):
-        rows = src.shape[0]
-        xv, xw = split(src[...].reshape(rows * RING, C))
+        rows, columns = src.shape[:2]
+        xv, xw = split(src[...].reshape(rows * columns, C))
         kh, kl = split(skipk[which])
         dot = functools.partial(jnp.dot, preferred_element_type=jnp.float32)
         term = dot(xv, kh) + (dot(xv, kl) + dot(xw, kh))
-        dst[...] = term.reshape(rows, RING, C)
+        dst[...] = term.reshape(rows, columns, C)
 
     ea[...] = jnp.zeros_like(ea)
     eb[...] = jnp.zeros_like(eb)
@@ -213,7 +244,7 @@
 
     def forward_b():
         return pltpu.make_async_remote_copy(
-            src_ref=h1.at[4:8],
+            src_ref=h1.at[4:8, 0:TILE],
             dst_ref=skb,
             send_sem=ssend.at[1],
             recv_sem=srecv.at[1],
@@ -224,29 +255,32 @@
     @pl.when(m > mirror)
     def _():
         forward_a().wait_recv()
-        skip_term(ska, ea, jnp.maximum(2 * (m - mirror), 0))
-
-    @pl.when(m >= mirror)
-    def _():
+        skip_term(ska, ea, 0)
+
+    def second_skip():
         forward_b().wait_recv()
-        skip_term(skb, eb, jnp.maximum(2 * (m - mirror) + 1, 0))
+        skip_term(skb, eb, 1)
+
+    @pl.when(m > mirror)
+    def _():
+        second_skip()
 
     def handover(d, kind):
         slot = 1 - d
         if kind == 0:
             src = yout
             dst = xbuf.at[4 * slot : 4 * slot + 4, 0:TILE, :]
-            row = r + 2 * d
+            seg = s + 2
         else:
-            src = yout.at[:, pl.ds(pl.multiple_of((TILE - STRIP) * (1 - half), STRIP), STRIP), :]
-            dst = xbuf.at[4 * slot : 4 * slot + 4, TILE:RING, :]
-            row = r + 1 - 2 * half + 2 * d
+            src = sout
+            dst = sin.at[4 * slot : 4 * slot + 4]
+            seg = s + 3 - 2 * c
         return pltpu.make_async_remote_copy(
             src_ref=src,
             dst_ref=dst,
             send_sem=msend.at[2 * (d + 1) + kind],
             recv_sem=mrecv.at[2 * slot + kind],
-            device_id=(s + 2, row),
+            device_id=(seg, r + 2 * d),
             device_id_type=MESH,
         )
 
@@ -277,19 +311,20 @@
 
     for q in (0, 1):
 
-        @pl.when((m == 0) & (half == q))
+        @pl.when((m == 0) & (slab == q))
         def _():
-            strip = TILE if q == 0 else TILE - STRIP
-            xbuf[4 + 2 * q : 6 + 2 * q, 0:TILE, :] = img[c, :, TILE * q : TILE * q + TILE, :]
-            xbuf[4 + 2 * q : 6 + 2 * q, TILE:RING, :] = img[c, :, strip : strip + STRIP, :]
-
-    @pl.when((m > 0) & (m < mirror))
-    def _():
-        forward_a().start()
+            xbuf[4 + 2 * q : 6 + 2 * q, 0:TILE, :] = img[q, :, own, :]
+            xbuf[4 + 2 * q : 6 + 2 * q, TILE:RING, :] = img[q, :, strip, :]
+
+    @pl.when(m > 0)
+    def _():
+        xbuf[:, TILE : TILE + 4] = sin[...]
+        xbuf[:, TILE + 4 : RING] = sin[...]
 
     @pl.when(m == mirror)
     def _():
         skip_term(xbuf.at[2:10], ea, 0)
+        second_skip()
 
     def conv(high, low, first, rows, slot, which):
         def part(ref, a):
@@ -328,32 +363,44 @@
     h1[2:10] = value
     store_split(xh, xl, 2, value)
 
-    @pl.when(m < mirror)
+    @pl.when(m == mirror - 1)
     def _():
         forward_b().start()
 
     hidden = inside_rows(silu(vec(1, 0) * conv(xh, xl, 3, 6, 1, 0) + vec(1, 1)), 3)
     store_split(hh, hl, 3, hidden)
-    value = h1[4:8] + silu(vec(1, 2) * (conv(hh, hl, 4, 4, 1, 1) + eb[...]) + vec(1, 3))
-    value = value[:, 0:TILE]
+    second = conv(hh, hl, 4, 4, 1, 1)[:, 0:TILE] + eb[...]
+    value = h1[4:8, 0:TILE] + silu(vec(1, 2) * second + vec(1, 3))
+
+    def handovers(action):
+        for d, kind in ((-1, 1), (1, 1), (-1, 0), (1, 0), (0, 1), (0, 0)):
+
+            @pl.when(inside[d])
+            def _():
+                action(handover(d, kind))
 
     @pl.when(m < stages - 1)
     def _():
         yout[...] = value
-        for kind in (0, 1):
-            for d in (-1, 1, 0):
-
-                @pl.when(inside[d])
-                def _():
-                    handover(d, kind).start()
+        sout[...] = jnp.where(c == 0, value[:, TILE - 4 :], value[:, :4])
+        handovers(lambda copy: copy.start())
+        handovers(lambda copy: copy.wait_send())
+
+    @pl.when((m > 0) & (m < mirror))
+    def _():
+        forward_a().start()
+
+    @pl.when(m < mirror - 1)
+    def _():
+        forward_b().start()
 
     def scatter(i, p):
         return pltpu.make_async_remote_copy(
             src_ref=fin.at[i, 2 * p : 2 * p + 2],
-            dst_ref=landed.at[c],
+            dst_ref=landed.at[slab],
             send_sem=fsend.at[2 * i + p],
-            recv_sem=frecv.at[c],
-            device_id=(pieces * half + i, 2 * g + p),
+            recv_sem=frecv.at[slab],
+            device_id=(pieces * c + i, 2 * g + p),
             device_id_type=MESH,
         )
 
@@ -361,7 +408,7 @@
         for i in range(pieces):
             for p in (0, 1):
 
-                @pl.when((pieces * half + i != s) | (2 * g + p != r))
+                @pl.when((pieces * c + i != s) | (2 * g + p != r))
                 def _():
                     action(scatter(i, p))
 
@@ -371,13 +418,15 @@
             fin[i] = value[:, i * cw : (i + 1) * cw, :]
         each_piece(lambda copy: copy.start())
 
-        @pl.when(half == 1)
-        def _():
-            landed[c] = fin[pieces - 2 + c, 2:4]
+        for p in (0, 1):
+
+            @pl.when((c == 1) & (slab == p))
+            def _():
+                landed[p] = fin[pieces - 1, 2 * p : 2 * p + 2]
 
     for k in (0, 1):
 
-        @pl.when((s != n_seg - 2 + k) | (r != source))
+        @pl.when((s != source) | (r != 2 * g + k))
         def _():
             pltpu.make_async_remote_copy(
                 src_ref=fin.at[0, 0:2],
@@ -394,15 +443,6 @@
         copy.wait_send()
     gathers(False)
 
-    @pl.when(m < stages - 1)
-    def _():
-        for kind in (0, 1):
-            for d in (-1, 0, 1):
-
-                @pl.when(inside[d])
-                def _():
-                    handover(d, kind).wait_send()
-
     @pl.when((m > 0) & (m < mirror))
     def _():
         forward_a().wait_send()
@@ -429,9 +469,16 @@
         return pl.pallas_call(
             functools.partial(level_kernel, n_seg, n_row),
             out_shape=jax.ShapeDtypeStruct((2, 2, cw, C), f32),
-            in_specs=[vmem] * 8,
+            in_specs=[pl.BlockSpec(memory_space=pl.ANY)] * 8,
             out_specs=vmem,
             scratch_shapes=[
+                pltpu.VMEM((2, 2, 2 * TILE, C), f32),
+                pltpu.VMEM((1, 3, 3, C, C), f32),
+                pltpu.VMEM((1, 3, 3, C, C), f32),
+                pltpu.VMEM((2, C, C), f32),
+                pltpu.VMEM((4, 1, C), f32),
+                pltpu.VMEM((4, 4, C), f32),
+                pltpu.VMEM((12, 4, C), f32),
                 pltpu.VMEM((12, RING, C), f32),
                 pltpu.VMEM((12, RING, C), f32),
                 pltpu.VMEM((12, RING, C), f32),
@@ -447,13 +494,13 @@
                 pltpu.VMEM((2, 4, 1, C), f32),
                 pltpu.VMEM((2, 2, 9 * C, 3 * C), f32),
                 pltpu.VMEM((8, RING, C), f32),
-                pltpu.VMEM((4, RING, C), f32),
+                pltpu.VMEM((4, TILE, C), f32),
                 pltpu.VMEM((8, RING, C), f32),
-                pltpu.VMEM((4, RING, C), f32),
+                pltpu.VMEM((4, TILE, C), f32),
                 pltpu.VMEM((RING, C), f32),
                 pltpu.VMEM((RING, C), f32),
-                dma((6,)),
-                dma((6,)),
+                dma((3,)),
+                dma((3,)),
                 dma((12,)),
                 dma((12,)),
                 dma((6,)),
@@ -462,9 +509,10 @@
                 dma((2,)),
                 dma((2 * pieces,)),
                 dma((2,)),
+                dma((8,)),
             ],
             compiler_params=pltpu.CompilerParams(
-                collective_id=0, has_side_effects=True, vmem_limit_bytes=48 * 1024 * 1024
+                collective_id=0, has_side_effects=True, vmem_limit_bytes=60 * 1024 * 1024
             ),
         )(*args)
 

time: 97 us -> 90.3 us (0.931)
  local copies, waits for them, and re-layouts: 7.29 us -> 1.3 us
    unnamed x17 -> x1, local copies, waits for them, and re-layouts: 7.29 us -> 1.3 us
where the time goes in v2:
time: 90.3 us; the launch traced here: 90.2 us
  Pallas kernels  88.8 us (98%)
  local copies, waits for them, and re-layouts  1.3 us (1%)
    pallas_call x1, Pallas kernels, on_device(): pl.pallas_call(functools.partial(level_kernel, n_seg, n_row), out_shape=j...  88.8 us

profile of v2, /device:TPU:1, one launch (start us, length us, event | category | flops | bytes accessed | tf_op | source)
XLA Modules:
  0.0 90.2 jit_solution(3907849060448944486)
XLA Ops:
  0.0 88.8 %shard_map.82 = f32[2,2,4,128]{3,2,1,0:T(4,128)} custom-call(f32[2,2,64,128]{3,2,1,0:T(8,128)} %img_hbm.1, f32[1,3,3,128,128]{4,3,2,1,0:T(8,128)} %w1_hbm.1, f32[1,3,3,128,128]{4,3,2,1,0:T(8,128)} %w2_hbm.1, f32[8,128,128]{2,1,0:T(8,128)} %skipk_hbm.1, f32[1,128]{1,0:T(1,128)} %g1_hbm.1, f32[1,128]{1,0:T(1,128)} %b1_hbm.1, f32[1,128]{1,0:T(1,128)} %g2_hbm.1, ...), custom_call_target="tpu_custom_call" | custom-call | tf_op jit(solution)/shard_map/pallas_call | solution.py:469
  88.9 1.3 %copy.10 = f32[2,2,4,128]{3,2,1,0:T(4,128)} copy(f32[2,2,4,128]{3,2,1,0:T(4,128)} %shard_map.82) | data formatting | bytes 16384

commit v3 on v2

--- a/solution.py
+++ b/solution.py
@@ -76,6 +76,7 @@
 ):
     stages = n_seg // 2
     mirror = stages // 2
+    relayed = mirror > 1
     groups = n_row // 2
     pieces = n_seg // 2
     cw = 2 * TILE // n_seg
@@ -126,7 +127,12 @@
             other = 2 * (g + d) + q
             greet(inside[d] & (m == 0) & (other != r), s, other)
     greet(m > mirror, 2 * (stages - m) + c, r)
-    greet(m >= mirror, 2 * (stages - 1 - m) + c, r)
+    if relayed:
+        greet((m >= mirror) & (m < stages - 1), 2 * (stages - 1 - m) + c, r)
+        greet(m == stages - 1, 2 + c, r)
+        greet(m == 1, c, r)
+    else:
+        greet(m >= mirror, 2 * (stages - 1 - m) + c, r)
     source = n_seg - 2 + s // pieces
     for k in (0, 1):
         greet((s != source) | (r != 2 * g + k), source, 2 * g + k)
@@ -139,6 +145,7 @@
         + jnp.where(m == 0, 2 * valid - 1, zero)
         + jnp.where((m > 0) & (m < mirror), one, zero)
         + jnp.where(m < mirror, one, zero)
+        + (jnp.where(m == 1, one, zero) if relayed else zero)
         + jnp.where(m == stages - 1, 2 * pieces - c, zero)
     )
     pl.semaphore_wait(barrier, expected)
@@ -248,7 +255,20 @@
             dst_ref=skb,
             send_sem=ssend.at[1],
             recv_sem=srecv.at[1],
-            device_id=(2 * (stages - 1 - m) + c, r),
+            device_id=(
+                jnp.where(m == 0, 2, 2 * (stages - 1 - m)) + c if relayed else s + 2,
+                r,
+            ),
+            device_id_type=MESH,
+        )
+
+    def relay():
+        return pltpu.make_async_remote_copy(
+            src_ref=skb,
+            dst_ref=skb,
+            send_sem=ssend.at[2],
+            recv_sem=srecv.at[1],
+            device_id=(2 * (stages - 1) + c, r),
             device_id_type=MESH,
         )
 
@@ -257,13 +277,10 @@
         forward_a().wait_recv()
         skip_term(ska, ea, 0)
 
-    def second_skip():
+    @pl.when(m >= mirror)
+    def _():
         forward_b().wait_recv()
         skip_term(skb, eb, 1)
-
-    @pl.when(m > mirror)
-    def _():
-        second_skip()
 
     def handover(d, kind):
         slot = 1 - d
@@ -324,7 +341,6 @@
     @pl.when(m == mirror)
     def _():
         skip_term(xbuf.at[2:10], ea, 0)
-        second_skip()
 
     def conv(high, low, first, rows, slot, which):
         def part(ref, a):
@@ -393,6 +409,14 @@
     @pl.when(m < mirror - 1)
     def _():
         forward_b().start()
+
+    if relayed:
+
+        @pl.when(m == 1)
+        def _():
+            forward_b().wait_recv()
+            relay().start()
+            relay().wait_send()
 
     def scatter(i, p):
         return pltpu.make_async_remote_copy(
@@ -505,7 +529,7 @@
                 dma((12,)),
                 dma((6,)),
                 dma((6,)),
-                dma((2,)),
+                dma((3,)),
                 dma((2,)),
                 dma((2 * pieces,)),
                 dma((2,)),

time: 90.3 us -> 88.7 us (0.982); the launches traced: 90.2 us -> 87.4 us
  Pallas kernels: 88.8 us -> 86 us
    pallas_call x1, Pallas kernels: 88.8 us -> 86 us  [on_device(): pl.pallas_call(functools.partial(level_kernel, n_seg, n_row), out_shape=j...]
where the time goes in v3:
time: 88.7 us; the launch traced here: 87.4 us
  Pallas kernels  86 us (97%)
  local copies, waits for them, and re-layouts  1.3 us (1%)
    pallas_call x1, Pallas kernels, on_device(): pl.pallas_call(functools.partial(level_kernel, n_seg, n_row), out_shape=j...  86 us

profile of v3, /device:TPU:1, one launch (start us, length us, event | category | flops | bytes accessed | tf_op | source)
XLA Modules:
  0.0 87.4 jit_solution(10494312919015253213)
XLA Ops:
  0.0 86.0 %shard_map.82 = f32[2,2,4,128]{3,2,1,0:T(4,128)} custom-call(f32[2,2,64,128]{3,2,1,0:T(8,128)} %img_hbm.1, f32[1,3,3,128,128]{4,3,2,1,0:T(8,128)} %w1_hbm.1, f32[1,3,3,128,128]{4,3,2,1,0:T(8,128)} %w2_hbm.1, f32[8,128,128]{2,1,0:T(8,128)} %skipk_hbm.1, f32[1,128]{1,0:T(1,128)} %g1_hbm.1, f32[1,128]{1,0:T(1,128)} %b1_hbm.1, f32[1,128]{1,0:T(1,128)} %g2_hbm.1, ...), custom_call_target="tpu_custom_call" | custom-call | tf_op jit(solution)/shard_map/pallas_call | solution.py:493
  86.1 1.3 %copy.10 = f32[2,2,4,128]{3,2,1,0:T(4,128)} copy(f32[2,2,4,128]{3,2,1,0:T(4,128)} %shard_map.82) | data formatting | bytes 16384

commit v4 on v3

--- a/solution.py
+++ b/solution.py
@@ -20,7 +20,7 @@
 
 
 def silu(u):
-    return u / (1.0 + jnp.exp(-u))
+    return u * (0.5 + 0.5 * jnp.tanh(0.5 * u))
 
 
 def level_kernel(
@@ -90,6 +90,11 @@
     down = (g < groups - 1).astype(jnp.int32)
     valid = 1 + up + down
     inside = {-1: g > 0, 0: g >= 0, 1: g < groups - 1}
+    long_way = 2 * (g % 2) - 1
+
+    def within(d):
+        return (g + d >= 0) & (g + d < groups)
+
 
     def greet(cond, seg, row):
         @pl.when(cond)
@@ -170,13 +175,13 @@
     strip = pl.ds(pl.multiple_of(TILE - STRIP * c, STRIP), STRIP)
 
     def gathers(start):
-        for d in (-1, 1, 0):
+        for d in (long_way, -long_way, 0):
             for q in (0, 1):
                 other = 2 * (g + d) + q
                 offset = 2 * slab - 4 * d + 4
                 index = (2 * (1 - d) + slab) * 2
 
-                @pl.when((m == 0) & inside[d] & (other != r))
+                @pl.when((m == 0) & within(d) & (other != r))
                 def _():
                     for kind, (a, b) in enumerate(
                         (
@@ -286,11 +291,11 @@
         slot = 1 - d
         if kind == 0:
             src = yout
-            dst = xbuf.at[4 * slot : 4 * slot + 4, 0:TILE, :]
+            dst = xbuf.at[pl.ds(4 * slot, 4), 0:TILE, :]
             seg = s + 2
         else:
             src = sout
-            dst = sin.at[4 * slot : 4 * slot + 4]
+            dst = sin.at[pl.ds(4 * slot, 4)]
             seg = s + 3 - 2 * c
         return pltpu.make_async_remote_copy(
             src_ref=src,
@@ -389,9 +394,10 @@
     value = h1[4:8, 0:TILE] + silu(vec(1, 2) * second + vec(1, 3))
 
     def handovers(action):
-        for d, kind in ((-1, 1), (1, 1), (-1, 0), (1, 0), (0, 1), (0, 0)):
-
-            @pl.when(inside[d])
+        far = [(d, kind) for kind in (1, 0) for d in (long_way, -long_way)]
+        for d, kind in far + [(0, 1), (0, 0)]:
+
+            @pl.when(within(d))
             def _():
                 action(handover(d, kind))
 

time: 88.7 us -> 88.8 us (level)
  no operation moved by 1% of the time
where the time goes in v4:
time: 88.8 us; the launch traced here: 87.5 us
  Pallas kernels  86.2 us (97%)
  local copies, waits for them, and re-layouts  1.3 us (1%)
    pallas_call x1, Pallas kernels, on_device(): pl.pallas_call(functools.partial(level_kernel, n_seg, n_row), out_shape=j...  86.2 us

profile of v4, /device:TPU:1, one launch (start us, length us, event | category | flops | bytes accessed | tf_op | source)
XLA Modules:
  0.0 87.5 jit_solution(6276731077508754548)
XLA Ops:
  0.0 86.2 %shard_map.82 = f32[2,2,4,128]{3,2,1,0:T(4,128)} custom-call(f32[2,2,64,128]{3,2,1,0:T(8,128)} %img_hbm.1, f32[1,3,3,128,128]{4,3,2,1,0:T(8,128)} %w1_hbm.1, f32[1,3,3,128,128]{4,3,2,1,0:T(8,128)} %w2_hbm.1, f32[8,128,128]{2,1,0:T(8,128)} %skipk_hbm.1, f32[1,128]{1,0:T(1,128)} %g1_hbm.1, f32[1,128]{1,0:T(1,128)} %b1_hbm.1, f32[1,128]{1,0:T(1,128)} %g2_hbm.1, ...), custom_call_target="tpu_custom_call" | custom-call | tf_op jit(solution)/shard_map/pallas_call | solution.py:499
  86.2 1.3 %copy.10 = f32[2,2,4,128]{3,2,1,0:T(4,128)} copy(f32[2,2,4,128]{3,2,1,0:T(4,128)} %shard_map.82) | data formatting | bytes 16384
